TPU v7x, 128 devices: a whole 4x4x4 slice. The times are simulated.
128 devices in a mesh: node: 64 (over z, y, x), hand: 2 (over core).
Axes of the slice: x: 4, y: 4, z: 4, core: 2. Of those that a mesh axis runs over, the one named last changes fastest.
Arguments:
- ranges: bfloat16 [2048, 128, 1326], P('node', None, 'hand'), may hold values from 0.00019931793 to 0.0039978027
- strengths: int32 [2048, 1326], P('node'), may hold values from 0 to 399
- live_hands: int32 [2048, 1326], P('node'), may hold values 0 or 1
- pot_sizes: float32 [2048, 128], P('node'), may hold values from 1 to 16
- action_counts: int32 [2048], P('node'), may hold values from 1 to 8
- parents: int32 [2048], P('node'), may hold values from 0 to 255
- turn_counts: int32 [64], replicated, may hold values from 1 to 4
- root_reach: float32 [64, 2, 1326], P(None, None, 'hand'), may hold values from 0.01 to 1
Outputs:
- turn_values: float32 [64, 2, 1326], P('node', None, 'hand')
- exploitability: float32 [], replicated
All inputs are finite; a program needn't handle non-finite values. No bound on the sum of `live_hands` on one device may be relied on, other than what follows from the above.
Results may differ from a plain program's by a relative error of at most 0.0003.
Values may be sent and summed in bfloat16 or wider, within the bound.
A program may use at most 128 MiB of HBM per device.

v0:
```python
import functools

import jax
import jax.numpy as jnp
import numpy as np
from jax import lax
from jax.sharding import Mesh
from jax.sharding import PartitionSpec as P

ACT = 8
GROUPS = 8
TACT = 4
NODE = ("node_0", "node_1", "node_2")
NODE_HAND = ("node_0", "node_1", "node_2", "hand")


def cut_along(shard, dim, count):
    before, after = (shard.shape[:dim], shard.shape[dim + 1 :])
    return jnp.moveaxis(shard.reshape(*before, count, -1, *after), dim, 0)


def sent_and_summed(shard, axis, dim):
    count = lax.axis_size(axis)
    parts = lax.all_to_all(cut_along(shard, dim, count), axis, 0, 0, tiled=True)
    return jnp.sum(parts, axis=0)


def one_axis_at_a_time(shard, axes):
    return functools.reduce(lax.psum, axes, shard)


def card_pairs(wanted):
    first_list = []
    second_list = []
    for lower_card in range(52):
        for upper_card in range(lower_card + 1, 52):
            first_list.append(lower_card)
            second_list.append(upper_card)
    return (
        jnp.asarray(np.array(first_list[:wanted], dtype=np.int32)),
        jnp.asarray(np.array(second_list[:wanted], dtype=np.int32)),
    )


def pair_compat(row_first, row_second, col_first, col_second):
    shared = (row_first[:, None] == col_first[None, :]) | (
        row_first[:, None] == col_second[None, :]
    )
    shared = (
        shared
        | (row_second[:, None] == col_first[None, :])
        | (row_second[:, None] == col_second[None, :])
    )
    return jnp.where(shared, 0.0, 1.0).astype(jnp.float32)


def showdown_block(compat, packed):
    left_strength, left_live, right_strength, right_live, reach_block = packed
    signs = jnp.sign((left_strength[:, :, None] - right_strength[:, None, :]).astype(jnp.float32))
    matrix = (signs * compat[None] * left_live[:, :, None] * right_live[:, None, :]).astype(
        jnp.bfloat16
    )
    return jnp.einsum("nij,nlj->nli", matrix, reach_block, preferred_element_type=jnp.float32)


def river_from(raw_values, pots, legal):
    count = raw_values.shape[0]
    width = raw_values.shape[2]
    values = (raw_values * pots[:, :, None]).reshape(count, 2, GROUPS, ACT, width)
    usable = jnp.arange(ACT)[None, :] < legal[:, None]
    return jnp.where(usable[:, None, None, :, None], values, -1e30).max(axis=3).sum(axis=2)


def turn_best(sums, legal):
    hand_half = sums.shape[1] // 2
    shaped = sums.reshape(-1, TACT, 2, hand_half)
    usable = jnp.arange(TACT)[None, :] < legal[:, None]
    return jnp.where(usable[:, :, None, None], shaped, -1e30).max(axis=1)


def local(
    ranges, strengths, live_hands, pot_sizes, action_counts, parents, turn_counts, root_reach
):
    node_count, line_cols, hand_half = ranges.shape
    hands_all = strengths.shape[1]
    hand_start = lax.axis_index("hand") * hand_half
    first_card, second_card = card_pairs(hands_all)
    live_all = live_hands.astype(jnp.float32)
    blocks = node_count // 4

    def grouped(array):
        return array.reshape((blocks, 4) + array.shape[1:])

    row_first = lax.dynamic_slice_in_dim(first_card, hand_start, hand_half, 0)
    row_second = lax.dynamic_slice_in_dim(second_card, hand_start, hand_half, 0)
    row_strength = lax.dynamic_slice_in_dim(strengths, hand_start, hand_half, 1)
    row_live = lax.dynamic_slice_in_dim(live_all, hand_start, hand_half, 1)
    compat = pair_compat(row_first, row_second, first_card, second_card)

    def one_block(packed):
        return showdown_block(compat, packed)

    added = lax.map(
        one_block,
        (
            grouped(row_strength),
            grouped(row_live),
            grouped(strengths),
            grouped(live_all),
            grouped(lax.all_gather(ranges, "hand", axis=2, tiled=True)),
        ),
    )
    raw_values = added.reshape(jnp.zeros((node_count, line_cols, hand_half), jnp.float32).shape)
    river_best = river_from(raw_values, pot_sizes, action_counts)
    flat_best = river_best.reshape(node_count, 2 * hand_half)
    turns_all = turn_counts.shape[0]
    turns_mine = turns_all // lax.axis_size(NODE)
    turn_start = lax.axis_index(NODE) * turns_mine
    rows_mine = turns_mine * TACT
    targets = jnp.arange(rows_mine * lax.axis_size(NODE), dtype=jnp.int32)
    onehot = (parents[None, :] == targets[:, None]).astype(jnp.float32)
    mine = sent_and_summed(jnp.dot(onehot, flat_best, precision=lax.Precision.HIGHEST), NODE, 0)
    legal_mine = lax.dynamic_slice_in_dim(turn_counts, turn_start, turns_mine, 0)
    turn_values = turn_best(mine, legal_mine)
    reach_mine = lax.dynamic_slice_in_dim(root_reach, turn_start, turns_mine, 0)
    exploitability = one_axis_at_a_time(jnp.sum(reach_mine * turn_values), NODE_HAND)
    return (turn_values, exploitability)


def solution(mesh):
    split = Mesh(
        mesh.devices.reshape(4, 4, 4, mesh.shape["hand"]), ("node_0", "node_1", "node_2", "hand")
    )
    in_specs = (
        P(NODE, None, "hand"),
        P(NODE, None),
        P(NODE, None),
        P(NODE, None),
        P(NODE),
        P(NODE),
        P(),
        P(None, None, "hand"),
    )
    out_specs = (P(NODE, None, "hand"), P())
    return jax.shard_map(local, mesh=split, in_specs=in_specs, out_specs=out_specs, check_vma=False)
```

profile of v0, /device:TPU:1, one launch (start us, length us, event | category | flops | bytes accessed | tf_op | source)
XLA Modules:
  0.0 228.3 jit_solution(14435566055462864649)
XLA Ops:
  7.2 0.7 all-gather.2.cloned.1.call-update
  8.0 0.9 convert_element_type.10
  9.1 1.0 reshape.101
  10.1 1.0 constant_dynamic-slice_fusion.2
  11.1 0.8 dynamic_slice.40
  11.9 0.8 dynamic_slice.41
  12.7 0.8 copy.24
  13.7 25.3 %all-gather.2.cloned.1.call-done = bf16[32,128,1326]{1,0,2:T(8,128)(2,1)} async-done(((bf16[32,128,663]{1,0,2:T(8,128)(2,1)}), bf16[32,128,1326]{1,0,2:T(8,128)(2,1)}) %all-gather.2.cloned.1.call-update) | async-done | bytes 10862608 | tf_op jit(solution)/shard_map/all_gather | solution.py:110
  39.1 84.1 %while.11 = (s32[]{:T(128)}, f32[8,4,128,663]{2,3,1,0:T(8,128)}, bf16[8,4,128,1326]{2,1,0,3:T(4,128)(2,1)}, s32[8,4,663]{2,1,0:T(4,128)S(1)}, s32[8,4,1326]{2,1,...) while((s32[]{:T(128)}, f32[8,4,128,663]{2,3,1,0:T(8,128)}, ...), condition=%wide.region_1.2_spmd.clone, body=%wide.region_0.1_spmd.clone.sunk | while | flops 931886272 | bytes 12673953 | solution.py:103
  39.1 1.6 constant_dynamic-slice_fusion.4
  40.7 1.5 or_select_fusion.2
  42.3 7.3 %fusion.11 = f32[8,4,128,663]{2,3,1,0:T(8,128)} fusion(f32[8,4,128,663]{2,3,1,0:T(8,128)} %get-tuple-element.197, s32[]{:T(128)} %get-tuple-element.196, f32[4,1326]{1,0:T(4,128)S(1)} %dynamic-slice_bitcast_fusion.8, f32[4,663]{1,0:T(4,128)S(1)} %dynamic-slice_bitcast_fusion.9, f32[663,1326]{1,0:T(8,128)S(1)} %or_select_fusion.2, ...), kind=kOutput, calls=%fused_computation.5.clone.1 | convolution fusion | flops 924853184 | bytes 6298408 | tf_op jit(solution)/shard_map/while/body/eval_jaxpr/nij,nlj->nli/dot_general | solution.py:63
  49.6 1.6 constant_dynamic-slice_fusion.4
  51.3 1.5 or_select_fusion.2
  52.8 7.3 %fusion.11 = f32[8,4,128,663]{2,3,1,0:T(8,128)} fusion(f32[8,4,128,663]{2,3,1,0:T(8,128)} %get-tuple-element.197, s32[]{:T(128)} %get-tuple-element.196, f32[4,1326]{1,0:T(4,128)S(1)} %dynamic-slice_bitcast_fusion.8, f32[4,663]{1,0:T(4,128)S(1)} %dynamic-slice_bitcast_fusion.9, f32[663,1326]{1,0:T(8,128)S(1)} %or_select_fusion.2, ...), kind=kOutput, calls=%fused_computation.5.clone.1 | convolution fusion | flops 924853184 | bytes 6298408 | tf_op jit(solution)/shard_map/while/body/eval_jaxpr/nij,nlj->nli/dot_general | solution.py:63
  60.1 1.6 constant_dynamic-slice_fusion.4
  61.8 1.5 or_select_fusion.2
  63.3 7.3 %fusion.11 = f32[8,4,128,663]{2,3,1,0:T(8,128)} fusion(f32[8,4,128,663]{2,3,1,0:T(8,128)} %get-tuple-element.197, s32[]{:T(128)} %get-tuple-element.196, f32[4,1326]{1,0:T(4,128)S(1)} %dynamic-slice_bitcast_fusion.8, f32[4,663]{1,0:T(4,128)S(1)} %dynamic-slice_bitcast_fusion.9, f32[663,1326]{1,0:T(8,128)S(1)} %or_select_fusion.2, ...), kind=kOutput, calls=%fused_computation.5.clone.1 | convolution fusion | flops 924853184 | bytes 6298408 | tf_op jit(solution)/shard_map/while/body/eval_jaxpr/nij,nlj->nli/dot_general | solution.py:63
  70.6 1.6 constant_dynamic-slice_fusion.4
  72.3 1.5 or_select_fusion.2
  73.9 7.3 %fusion.11 = f32[8,4,128,663]{2,3,1,0:T(8,128)} fusion(f32[8,4,128,663]{2,3,1,0:T(8,128)} %get-tuple-element.197, s32[]{:T(128)} %get-tuple-element.196, f32[4,1326]{1,0:T(4,128)S(1)} %dynamic-slice_bitcast_fusion.8, f32[4,663]{1,0:T(4,128)S(1)} %dynamic-slice_bitcast_fusion.9, f32[663,1326]{1,0:T(8,128)S(1)} %or_select_fusion.2, ...), kind=kOutput, calls=%fused_computation.5.clone.1 | convolution fusion | flops 924853184 | bytes 6298408 | tf_op jit(solution)/shard_map/while/body/eval_jaxpr/nij,nlj->nli/dot_general | solution.py:63
  81.1 1.6 constant_dynamic-slice_fusion.4
  82.8 1.5 or_select_fusion.2
  84.3 7.3 %fusion.11 = f32[8,4,128,663]{2,3,1,0:T(8,128)} fusion(f32[8,4,128,663]{2,3,1,0:T(8,128)} %get-tuple-element.197, s32[]{:T(128)} %get-tuple-element.196, f32[4,1326]{1,0:T(4,128)S(1)} %dynamic-slice_bitcast_fusion.8, f32[4,663]{1,0:T(4,128)S(1)} %dynamic-slice_bitcast_fusion.9, f32[663,1326]{1,0:T(8,128)S(1)} %or_select_fusion.2, ...), kind=kOutput, calls=%fused_computation.5.clone.1 | convolution fusion | flops 924853184 | bytes 6298408 | tf_op jit(solution)/shard_map/while/body/eval_jaxpr/nij,nlj->nli/dot_general | solution.py:63
  91.7 1.6 constant_dynamic-slice_fusion.4
  93.3 1.5 or_select_fusion.2
  94.9 7.3 %fusion.11 = f32[8,4,128,663]{2,3,1,0:T(8,128)} fusion(f32[8,4,128,663]{2,3,1,0:T(8,128)} %get-tuple-element.197, s32[]{:T(128)} %get-tuple-element.196, f32[4,1326]{1,0:T(4,128)S(1)} %dynamic-slice_bitcast_fusion.8, f32[4,663]{1,0:T(4,128)S(1)} %dynamic-slice_bitcast_fusion.9, f32[663,1326]{1,0:T(8,128)S(1)} %or_select_fusion.2, ...), kind=kOutput, calls=%fused_computation.5.clone.1 | convolution fusion | flops 924853184 | bytes 6298408 | tf_op jit(solution)/shard_map/while/body/eval_jaxpr/nij,nlj->nli/dot_general | solution.py:63
  102.2 1.6 constant_dynamic-slice_fusion.4
  103.9 1.5 or_select_fusion.2
  105.4 7.3 %fusion.11 = f32[8,4,128,663]{2,3,1,0:T(8,128)} fusion(f32[8,4,128,663]{2,3,1,0:T(8,128)} %get-tuple-element.197, s32[]{:T(128)} %get-tuple-element.196, f32[4,1326]{1,0:T(4,128)S(1)} %dynamic-slice_bitcast_fusion.8, f32[4,663]{1,0:T(4,128)S(1)} %dynamic-slice_bitcast_fusion.9, f32[663,1326]{1,0:T(8,128)S(1)} %or_select_fusion.2, ...), kind=kOutput, calls=%fused_computation.5.clone.1 | convolution fusion | flops 924853184 | bytes 6298408 | tf_op jit(solution)/shard_map/while/body/eval_jaxpr/nij,nlj->nli/dot_general | solution.py:63
  112.7 1.6 constant_dynamic-slice_fusion.4
  114.3 1.5 or_select_fusion.2
  115.9 7.3 %fusion.11 = f32[8,4,128,663]{2,3,1,0:T(8,128)} fusion(f32[8,4,128,663]{2,3,1,0:T(8,128)} %get-tuple-element.197, s32[]{:T(128)} %get-tuple-element.196, f32[4,1326]{1,0:T(4,128)S(1)} %dynamic-slice_bitcast_fusion.8, f32[4,663]{1,0:T(4,128)S(1)} %dynamic-slice_bitcast_fusion.9, f32[663,1326]{1,0:T(8,128)S(1)} %or_select_fusion.2, ...), kind=kOutput, calls=%fused_computation.5.clone.1 | convolution fusion | flops 924853184 | bytes 6298408 | tf_op jit(solution)/shard_map/while/body/eval_jaxpr/nij,nlj->nli/dot_general | solution.py:63
  123.2 12.0 %copy.23 = f32[8,4,128,663]{3,2,1,0:T(8,128)} copy(f32[8,4,128,663]{2,3,1,0:T(8,128)} %get-tuple-element.44) | data formatting | bytes 21725184 | tf_op jit(solution)/shard_map/while | solution.py:103
  135.1 16.8 %select_reduce_fusion = f32[32,2,8,663]{3,2,1,0:T(8,128)S(1)} fusion(f32[32,2,8,8,663]{4,3,2,1,0:T(8,128)} %bitcast.32, f32[32,2,8,8]{3,2,1,0:T(8,128)S(1)} %copy.25, pred[32,8]{1,0:T(8,128)(4,1)S(1)} %iota_compare_fusion), kind=kLoop, calls=%fused_computation.12 | loop fusion | flops 7807488 | bytes 12237056 | tf_op jit(solution)/shard_map/reduce_max | solution.py:71
  152.0 0.5 reduce_sum.27
  152.6 0.8 fusion.5
  153.5 2.0 copy.26
  155.5 10.1 %all-to-all-start = ((f32[64,4,1326]{2,1,0:T(4,128)}), f32[64,4,1326]{2,1,0:T(4,128)S(1)}, u32[]{:S(2)}, u32[]{:S(2)}) async-start(f32[64,4,1326]{2,1,0:T(4,128)} %copy.26), calls=%async_computation | async-start | bytes 2883584 | tf_op jit(solution)/shard_map/all_to_all | solution.py:24
  165.7 0.6 dynamic_slice.38
  166.3 0.6 iota_compare_fusion.1
  166.9 21.1 %all-to-all-done = f32[64,4,1326]{2,1,0:T(4,128)S(1)} async-done(((f32[64,4,1326]{2,1,0:T(4,128)}), f32[64,4,1326]{2,1,0:T(4,128)S(1)}, u32[]{:S(2)}, u32[]{:S(2)}) %all-to-all-start) | async-done | bytes 1357856 | tf_op jit(solution)/shard_map/all_to_all | solution.py:24
  188.0 0.3 reduce_sum.28
  188.5 1.3 multiply_reduce_fusion
  189.8 7.1 %psum.28 = f32[]{:T(128)} all-reduce(f32[]{:T(128)} %multiply_reduce_fusion), channel_id=1, replica_groups=mesh['node_0'=4,'node_1'=4,'node_2'=4,'hand'=2] {'node_0'}, use_global_device_ids=true, to_apply=%region_7.8 | all-reduce | flops 1 | bytes 8 | tf_op jit(solution)/shard_map/psum | solution.py:29
  196.9 7.5 %psum.29 = f32[]{:T(128)} all-reduce(f32[]{:T(128)} %psum.28), channel_id=1, replica_groups=mesh['node_0'=4,'node_1'=4,'node_2'=4,'hand'=2] {'node_1'}, use_global_device_ids=true, to_apply=%region_8.9 | all-reduce | flops 1 | bytes 8 | tf_op jit(solution)/shard_map/psum | solution.py:29
  204.4 6.9 %psum.30 = f32[]{:T(128)} all-reduce(f32[]{:T(128)} %psum.29), channel_id=1, replica_groups=mesh['node_0'=4,'node_1'=4,'node_2'=4,'hand'=2] {'node_2'}, use_global_device_ids=true, to_apply=%region_9.10 | all-reduce | flops 1 | bytes 8 | tf_op jit(solution)/shard_map/psum | solution.py:29
  211.3 10.2 %psum.31 = f32[]{:T(128)} all-reduce(f32[]{:T(128)} %psum.30), channel_id=1, replica_groups=mesh['node_0'=4,'node_1'=4,'node_2'=4,'hand'=2] {'hand'}, use_global_device_ids=true, to_apply=%region_10.11 | all-reduce | flops 1 | bytes 8 | tf_op jit(solution)/shard_map/psum | solution.py:29
  (56 shorter events, 1.2 us)
Async XLA Ops:
  7.2 31.9 %copy-start = (s32[1326]{0:T(1024)S(1)}, s32[1326]{0:T(1024)}, u32[]{:S(2)}) copy-start(s32[1326]{0:T(1024)} %constant.58.clone) | copy-start | bytes 15916
  7.2 31.9 %copy-start.1 = (s32[1326]{0:T(1024)S(1)}, s32[1326]{0:T(1024)}, u32[]{:S(2)}) copy-start(s32[1326]{0:T(1024)} %constant.59.clone) | copy-start | bytes 15916
  7.2 6.5 %copy-start.4 = (s32[32]{0:T(128)S(1)}, s32[32]{0:T(128)}, u32[]{:S(2)}) copy-start(s32[32]{0:T(128)} %param.16) | copy-start | bytes 388
  7.2 31.9 %all-gather.2.cloned.1.call-start = ((), (), s32[]{:S(2)}) async-start(), calls=%async_computation.1 | async-start | bytes 16293888 | tf_op jit(solution)/shard_map/all_gather | solution.py:110
  135.1 17.5 %copy-start.3 = (s32[32]{0:T(128)S(1)}, s32[32]{0:T(128)}, u32[]{:S(2)}) copy-start(s32[32]{0:T(128)} %param.17) | copy-start | bytes 388
  152.0 13.7 %copy-start.5 = (s32[64]{0:T(128)S(1)}, s32[64]{0:T(128)}, u32[]{:S(2)}) copy-start(s32[64]{0:T(128)} %param.18) | copy-start | bytes 772
  155.5 32.5 %all-to-all-start = ((f32[64,4,1326]{2,1,0:T(4,128)}), f32[64,4,1326]{2,1,0:T(4,128)S(1)}, u32[]{:S(2)}, u32[]{:S(2)}) async-start(f32[64,4,1326]{2,1,0:T(4,128)} %copy.26), calls=%async_computation | async-start | bytes 2883584 | tf_op jit(solution)/shard_map/all_to_all | solution.py:24
  188.5 33.0 %copy-start.2 = (f32[1,2,663]{2,1,0:T(2,128)}, f32[1,2,663]{2,1,0:T(2,128)S(1)}, u32[]{:S(2)}) copy-start(f32[1,2,663]{2,1,0:T(2,128)S(1)} %reduce_max.22) | copy-start | bytes 15916
Sparse Core Ops, SparseCore 0:
  9.7 29.3 all-gather.1
where the time goes:
time: 229 us; the launch traced here: 228 us
  matrix products  59.2 us (26%)
  waiting for transfers between devices  47.1 us (21%)
  other arithmetic  32.8 us (14%)
  local copies, waits for them, and re-layouts  32.7 us (14%)
  blocking collectives  31.7 us (14%)
  between operations  14.2 us (6%)
  starting transfers between devices  10.2 us (4%)
    dot_general x8, matrix products, showdown_block(): jnp.einsum('nij,nlj->nli', matrix, reach_block, preferred_element_type=jn...  58.4 us
    psum x4, blocking collectives, one_axis_at_a_time(): return functools.reduce(lax.psum, axes, shard)  31.7 us
    all_gather x1, waiting for transfers between devices, local(): lax.all_gather(ranges, 'hand', axis=2, tiled=True)  25.3 us
    all_to_all x1, waiting for transfers between devices, sent_and_summed(): parts = lax.all_to_all(cut_along(shard, dim, count), axis, 0, 0, tiled=True)  21.1 us
    reduce_max x1, other arithmetic, river_from(): jnp.where(usable[:, None, None, :, None], values, -1e+30).max(axis=3)  16.8 us
    dynamic_slice x8, local copies, waits for them, and re-layouts, local(): lax.map(one_block, (grouped(row_strength), grouped(row_live), grouped(str...  12.8 us
    select_n x8, other arithmetic, pair_compat(): return jnp.where(shared, 0.0, 1.0).astype(jnp.float32)  12.2 us
    while x1, local copies, waits for them, and re-layouts, local(): lax.map(one_block, (grouped(row_strength), grouped(row_live), grouped(str...  12 us
  transfers between devices with their start and end apart: 2, of which 2 were waited for; matrix products, arithmetic and copies ran while one was open for 3% of the time, Pallas kernels for 0%

commit v1 on v0

v1 whole, which is shorter than its diff:
```python
import functools

import jax
import jax.numpy as jnp
import numpy as np
from jax import lax
from jax.experimental import pallas as pl
from jax.experimental.pallas import tpu as pltpu
from jax.sharding import Mesh
from jax.sharding import PartitionSpec as P

AXES = ("node_0", "node_1", "node_2", "hand")
NODE = AXES[:3]
MESH_ID = pl.DeviceIdType.MESH
F32 = jnp.float32
BF16 = jnp.bfloat16

ACT = 8
GROUPS = 8
TACT = 4
LINES = 128
HALF = 663
WIDE = 768
LOCAL = 32
MINE = 16
EARLY = 11
K_TILES = ((0, 256, 256), (256, 256, 256), (512, 160, 151))


def card_rows():
    first, second = np.triu_indices(52, 1)
    rows = np.zeros((8, WIDE), np.float32)
    for half in range(2):
        part = slice(half * HALF, (half + 1) * HALF)
        rows[half, :HALF] = first[part]
        rows[2 + half, :HALF] = second[part]
    return rows


def tall(row, rows):
    width = row.shape[1]
    block = jnp.broadcast_to(row, (16, width)).astype(BF16)
    return jnp.broadcast_to(block[None], (rows // 16, 16, width)).reshape(rows, width)


def turned(row):
    return jnp.broadcast_to(row, (128, 128)).T


def kernel(
    sizes,
    ranges,
    strengths,
    live,
    pots,
    counts,
    parents,
    turn_counts,
    reach,
    cards,
    turn_out,
    total_out,
    own_ranges,
    other_ranges,
    masked,
    s_rows,
    live_rows,
    pot_rows,
    s_columns,
    allow,
    forbid,
    partial,
    gathered,
    outgoing,
    keys,
    sums,
    arrived,
    my_reach,
    plane_part,
    plane_got,
    line_part,
    line_got,
    own_sem,
    other_sem,
    ranges_send,
    line_recv,
    line_send,
    key_recv,
    key_send,
    plane_recv,
    plane_send,
    reach_sem,
    b1_recv,
    b1_send,
    b2_recv,
    b2_send,
):
    place = [lax.axis_index(name) for name in NODE]
    core = lax.axis_index("hand")
    far = 1 - core
    turn = (place[0] * sizes[1] + place[1]) * sizes[2] + place[2]
    planes = ((1, 2), (0, 2), (0, 1))

    def at(where, which):
        return (where[0], where[1], where[2], which)

    def along(axis, step):
        where = list(place)
        where[axis] = lax.rem(place[axis] + step, sizes[axis])
        return where

    def plane_size(axis):
        high, low = planes[axis]
        return sizes[high] * sizes[low]

    def plane_mine(axis):
        high, low = planes[axis]
        return place[high] * sizes[low] + place[low]

    def in_plane(axis, slot):
        high, low = planes[axis]
        where = list(place)
        where[high] = slot // sizes[low]
        where[low] = lax.rem(slot, sizes[low])
        return where

    peers = [at(place, far)]
    for axis in range(3):
        for step in range(1, sizes[axis]):
            peers += [at(along(axis, step), which) for which in (core, far)]
    for axis in range(3):
        high, low = planes[axis]
        for up in range(1, sizes[high]):
            for side in range(1, sizes[low]):
                where = list(place)
                where[high] = lax.rem(place[high] + up, sizes[high])
                where[low] = lax.rem(place[low] + side, sizes[low])
                peers.append(at(where, core))

    barrier = pltpu.get_barrier_semaphore()
    for peer in peers:
        pl.semaphore_signal(barrier, inc=1, device_id=peer, device_id_type=MESH_ID)

    first = core * MINE
    for n in range(MINE):
        pltpu.make_async_copy(ranges.at[first + n], own_ranges.at[n], own_sem.at[n]).start()
    pltpu.make_async_copy(reach.at[turn], my_reach, reach_sem).start()

    rows = pl.ds(pl.multiple_of(first, MINE), MINE)
    s_rows[...] = jnp.zeros_like(s_rows)
    live_rows[...] = jnp.zeros_like(live_rows)
    for source, target, shift in ((strengths, s_rows, 200.0), (live, live_rows, 0.0)):
        low = source[rows, 0:HALF].astype(F32) - shift
        high = source[rows, HALF : 2 * HALF].astype(F32) - shift
        mine, theirs = jnp.where(core == 0, low, high), jnp.where(core == 0, high, low)
        for n in range(MINE):
            target[0, n, :, 0:HALF] = mine[n : n + 1]
            target[1, n, :, 0:HALF] = theirs[n : n + 1]
    my_pots = pots[rows, :]
    for n in range(MINE):
        pot_rows[n] = my_pots[n : n + 1]

    def pick(kind, half, lanes):
        low = cards[pl.ds(2 * kind, 1), lanes]
        high = cards[pl.ds(2 * kind + 1, 1), lanes]
        return jnp.where(core == half, low, high)

    lane = lax.broadcasted_iota(jnp.int32, (128, 128), 1)
    inside = (lane < HALF - 640).astype(F32).astype(BF16)

    def build(block, _):
        j_lanes = pl.ds(pl.multiple_of(block * 128, 128), 128)
        for j_half in range(2):
            a = turned(pick(0, j_half, j_lanes)).astype(BF16)
            b = turned(pick(1, j_half, j_lanes)).astype(BF16)
            for i_half in range(2):
                for i_block in range(6):
                    lanes = pl.ds(i_block * 128, 128)
                    c = tall(pick(0, i_half, lanes), 128)
                    d = tall(pick(1, i_half, lanes), 128)
                    apart = ((a - c) * (a - d)) * ((b - c) * (b - d))
                    one = jnp.minimum(jnp.abs(apart), jnp.ones_like(apart))
                    if i_block == 5:
                        one = one * inside
                    where = pl.ds(i_half * WIDE + i_block * 128, 128)
                    allow[j_half, j_lanes, where] = one
                    forbid[j_half, j_lanes, where] = -one
        return 0

    lax.fori_loop(0, 6, build, 0)

    def prepare(half, source, n):
        for block in range(6):
            lanes = pl.ds(block * 128, 128)
            s_columns[lanes, :] = turned(s_rows[half, n, :, lanes]).astype(BF16)
        for start, _, width in K_TILES:
            lanes = pl.ds(start, width)
            flags = tall(live_rows[half, n, :, lanes], LINES)
            masked[:, lanes] = source[n, :, lanes] * flags

    def product(half, n, tile):
        lanes = pl.ds((tile % 3) * 256, 256)
        s_lane = s_rows[tile // 3, n, :, lanes]
        added = None
        for start, tall_rows, width in K_TILES:
            inner = pl.ds(start, tall_rows)
            column = s_columns[inner, :]
            gap = tall(s_lane, tall_rows) - jnp.concatenate([column, column], axis=1)
            where = pl.ds(tile * 256, 256)
            sign = jnp.minimum(
                jnp.maximum(gap, forbid[half, inner, where]), allow[half, inner, where]
            )
            term = jnp.dot(
                masked[:, pl.ds(start, width)], sign[:width], preferred_element_type=F32
            )
            added = term if added is None else added + term
        return added

    def own_half(n, _):
        pltpu.make_async_copy(ranges.at[first + n], own_ranges.at[n], own_sem.at[n]).wait()
        prepare(0, own_ranges, n)
        for tile in range(6):
            partial[n, :, pl.ds(tile * 256, 256)] = product(0, n, tile)
        return 0

    def exchange(n):
        return pltpu.make_async_remote_copy(
            src_ref=ranges.at[far * MINE + n],
            dst_ref=other_ranges.at[n],
            send_sem=ranges_send.at[n],
            recv_sem=other_sem.at[n],
            device_id=at(place, far),
            device_id_type=MESH_ID,
        )

    lax.fori_loop(0, EARLY, own_half, 0)
    pl.semaphore_wait(barrier, len(peers))
    for n in range(MINE):
        exchange(n).start()

    lane_row = lax.broadcasted_iota(jnp.int32, (1, 128), 1)
    spread = jnp.zeros((1, 128), jnp.int32)
    for n in range(LOCAL):
        spread = jnp.where(lane_row // 4 == n, parents[n], spread)
    key_row = (spread * 4 + lax.rem(lane_row, 4)).astype(F32)

    def key_copy(axis, step):
        return pltpu.make_async_remote_copy(
            src_ref=keys.at[axis, 0],
            dst_ref=keys.at[axis, sizes[axis] - step],
            send_sem=key_send.at[axis, step],
            recv_sem=key_recv.at[axis, sizes[axis] - step],
            device_id=at(along(axis, step), core),
            device_id_type=MESH_ID,
        )

    for axis in range(3):
        keys[axis, 0] = key_row
        for step in range(1, sizes[axis]):
            key_copy(axis, step).start()

    lax.fori_loop(EARLY, MINE, own_half, 0)

    my_block = core * (MINE * 4)

    def river_copies(batch):
        copies = []
        from_rows = pl.ds(pl.multiple_of(batch * 8, 8), 8)
        mine = pl.ds(pl.multiple_of(my_block + batch * 8, 8), 8)
        for axis in range(3):
            send, recv = line_send.at[axis], line_recv.at[axis]
            for step in range(1, sizes[axis]):
                base = (sizes[axis] - step) * 128
                there = pl.ds(pl.multiple_of(base + my_block + batch * 8, 8), 8)
                for source, which in (
                    (gathered.at[axis, mine], core),
                    (outgoing.at[axis, from_rows], far),
                ):
                    copies.append(
                        pltpu.make_async_remote_copy(
                            src_ref=source,
                            dst_ref=gathered.at[axis, there],
                            send_sem=send,
                            recv_sem=recv,
                            device_id=at(along(axis, step), which),
                            device_id_type=MESH_ID,
                        )
                    )
            copies.append(
                pltpu.make_async_remote_copy(
                    src_ref=outgoing.at[axis, from_rows],
                    dst_ref=gathered.at[axis, mine],
                    send_sem=send,
                    recv_sem=recv,
                    device_id=at(place, far),
                    device_id_type=MESH_ID,
                )
            )
        return copies

    action = lax.rem(lax.broadcasted_iota(jnp.int32, (LINES, 256), 0), ACT)

    def other_half(n):
        exchange(n).wait_recv()
        prepare(1, other_ranges, n)
        usable = action < counts[first + n]
        pot = turned(pot_rows[n])
        pot = jnp.concatenate([pot, pot], axis=1)
        rivers = []
        for tile in range(6):
            values = product(1, n, tile) + partial[n, :, pl.ds(tile * 256, 256)]
            values = jnp.where(usable, values * pot, -1e30)
            best = values.reshape(2, GROUPS, ACT, 256).max(axis=2).sum(axis=1)
            best = best * live_rows[tile // 3, n, :, pl.ds((tile % 3) * 256, 256)]
            rivers.append(best)
        return rivers

    def two_nodes(batch, _):
        even, odd = other_half(2 * batch), other_half(2 * batch + 1)
        for tile in range(6):
            pieces = []
            for best in (even[tile], odd[tile]):
                for player in range(2):
                    for side in range(2):
                        lanes = slice(side * 128, side * 128 + 128)
                        pieces.append(best[player : player + 1, lanes])
            block = jnp.concatenate(pieces, axis=0)
            if tile < 3:
                gathered[tile, pl.ds(pl.multiple_of(my_block + batch * 8, 8), 8), :] = block
            else:
                outgoing[tile - 3, pl.ds(pl.multiple_of(batch * 8, 8), 8), :] = block
        for copy in river_copies(batch):
            copy.start()
        return 0

    lax.fori_loop(0, MINE // 2, two_nodes, 0)

    for axis in range(3):
        for step in range(1, sizes[axis]):
            key_copy(axis, step).wait_recv()

    for axis in range(3):
        count = plane_size(axis)
        q = lax.broadcasted_iota(jnp.int32, (count * 16, 128), 0)
        there = in_plane(axis, q // 16)
        owner = (there[0] * sizes[1] + there[1]) * sizes[2] + there[2]
        wanted = (owner * (TACT * 4) + lax.rem(q, 16)).astype(F32)
        lines = sizes[axis] * 128
        hot = jnp.concatenate(
            [
                jnp.where(wanted == keys[axis, e], 1.0, 0.0).astype(BF16)
                for e in range(sizes[axis])
            ],
            axis=1,
        )
        blocks = (sizes[axis] - 1) * 128 + 64
        whole = gathered.at[axis, pl.ds(0, blocks)]
        pltpu.make_async_copy(whole, whole, line_recv.at[axis]).wait()
        rows_in = gathered[axis, pl.ds(0, lines), :]
        upper = rows_in.astype(BF16)
        lower = (rows_in - upper.astype(F32)).astype(BF16)
        both = jnp.dot(hot, upper, preferred_element_type=F32) + jnp.dot(
            hot, lower, preferred_element_type=F32
        )
        sums[axis, pl.ds(0, count * 16), :] = both
        mine = plane_mine(axis)
        here = pl.ds(pl.multiple_of(mine * 16, 16), 16)
        for step in range(1, count):
            slot = lax.rem(mine + step, count)
            part = pl.ds(pl.multiple_of(slot * 16, 16), 16)
            pltpu.make_async_remote_copy(
                src_ref=sums.at[axis, part],
                dst_ref=arrived.at[axis, here],
                send_sem=plane_send.at[axis],
                recv_sem=plane_recv.at[axis],
                device_id=at(in_plane(axis, slot), core),
                device_id_type=MESH_ID,
            ).start()
        arrived[axis, here, :] = sums[axis, here, :]

    pltpu.make_async_copy(reach.at[turn], my_reach, reach_sem).wait()
    legal = turn_counts[turn]
    spot = lax.broadcasted_iota(jnp.int32, (1, 128), 1)
    weighed = jnp.zeros((1, 128), F32)
    for axis in range(3):
        count = plane_size(axis)
        whole = arrived.at[axis, pl.ds(0, (count - 1) * 16)]
        pltpu.make_async_copy(whole, whole, plane_recv.at[axis]).wait()
        total = arrived[axis, pl.ds(0, count * 16), :].reshape(count, 16, 128).sum(axis=0)
        best = total[0:4]
        for a in range(1, TACT):
            best = jnp.maximum(best, jnp.where(a < legal, total[4 * a : 4 * a + 4], -1e30))
        for player in range(2):
            for side in range(2):
                piece = best[player * 2 + side : player * 2 + side + 1]
                start = axis * 256 + side * 128
                width = min(128, HALF - start)
                lanes = pl.ds(start, width)
                turn_out[0, pl.ds(player, 1), lanes] = piece[:, :width]
                part = piece[:, :width] * my_reach[pl.ds(player, 1), lanes]
                if width == 128:
                    weighed = weighed + part
                else:
                    weighed = weighed + jnp.where(
                        spot == 0, jnp.sum(part, axis=1, keepdims=True), 0.0
                    )

    count = plane_size(2)
    mine = plane_mine(2)
    plane_part[0] = weighed
    plane_got[mine] = weighed

    def first_hop(step):
        slot = lax.rem(mine + step, count)
        return pltpu.make_async_remote_copy(
            src_ref=plane_part.at[0],
            dst_ref=plane_got.at[mine],
            send_sem=b1_send,
            recv_sem=b1_recv,
            device_id=at(in_plane(2, slot), core),
            device_id_type=MESH_ID,
        )

    for step in range(1, count):
        first_hop(step).start()
    whole = plane_got.at[pl.ds(0, count - 1)]
    pltpu.make_async_copy(whole, whole, b1_recv).wait()
    weighed = plane_got[...].sum(axis=0)
    slots = sizes[2] * 2
    slot = place[2] * 2 + core
    line_part[0] = weighed
    line_got[slot] = weighed

    def second_hop(step, which):
        return pltpu.make_async_remote_copy(
            src_ref=line_part.at[0],
            dst_ref=line_got.at[slot],
            send_sem=b2_send,
            recv_sem=b2_recv,
            device_id=at(along(2, step), which),
            device_id_type=MESH_ID,
        )

    second_hop(0, far).start()
    for step in range(1, sizes[2]):
        second_hop(step, core).start()
        second_hop(step, far).start()

    for n in range(MINE):
        exchange(n).wait_send()
    for axis in range(3):
        for step in range(1, sizes[axis]):
            key_copy(axis, step).wait_send()
        sent = gathered.at[axis, pl.ds(0, (sizes[axis] - 1) * 64)]
        for _ in range(2):
            pltpu.make_async_copy(sent, sent, line_send.at[axis]).wait()
        sent = gathered.at[axis, pl.ds(0, 64)]
        pltpu.make_async_copy(sent, sent, line_send.at[axis]).wait()
        sent = arrived.at[axis, pl.ds(0, (plane_size(axis) - 1) * 16)]
        pltpu.make_async_copy(sent, sent, plane_send.at[axis]).wait()
    sent = plane_got.at[pl.ds(0, count - 1)]
    pltpu.make_async_copy(sent, sent, b1_send).wait()
    sent = line_got.at[pl.ds(0, slots - 1)]
    pltpu.make_async_copy(sent, sent, b2_send).wait()
    pltpu.make_async_copy(sent, sent, b2_recv).wait()
    total_out[0, 0] = jnp.sum(line_got[...].sum(axis=0))


def local(sizes, ranges, strengths, live, pots, counts, parents, turn_counts, reach):
    dma = pltpu.SemaphoreType.DMA
    longest = max(sizes)
    widest = max(sizes[0] * sizes[1], sizes[1] * sizes[2], sizes[0] * sizes[2])
    vmem = pl.BlockSpec(memory_space=pltpu.VMEM)
    smem = pl.BlockSpec(memory_space=pltpu.SMEM)
    hbm = pl.BlockSpec(memory_space=pl.ANY)
    turn_values, total = pl.pallas_call(
        functools.partial(kernel, sizes),
        out_shape=(
            jax.ShapeDtypeStruct((1, 2, HALF), F32),
            jax.ShapeDtypeStruct((1, 1), F32),
        ),
        in_specs=[hbm, vmem, vmem, vmem, smem, smem, smem, hbm, vmem],
        out_specs=(vmem, smem),
        scratch_shapes=[
            pltpu.VMEM((MINE, LINES, HALF), BF16),
            pltpu.VMEM((MINE, LINES, HALF), BF16),
            pltpu.VMEM((LINES, HALF), BF16),
            pltpu.VMEM((2, MINE, 1, WIDE), F32),
            pltpu.VMEM((2, MINE, 1, WIDE), F32),
            pltpu.VMEM((MINE, 1, LINES), F32),
            pltpu.VMEM((WIDE, 128), BF16),
            pltpu.VMEM((2, WIDE, 2 * WIDE), BF16),
            pltpu.VMEM((2, WIDE, 2 * WIDE), BF16),
            pltpu.VMEM((MINE, LINES, 2 * WIDE), F32),
            pltpu.VMEM((3, longest * 128, 128), F32),
            pltpu.VMEM((3, 64, 128), F32),
            pltpu.VMEM((3, longest, 1, 128), F32),
            pltpu.VMEM((3, widest * 16, 128), F32),
            pltpu.VMEM((3, widest * 16, 128), F32),
            pltpu.VMEM((2, HALF), F32),
            pltpu.VMEM((1, 1, 128), F32),
            pltpu.VMEM((sizes[0] * sizes[1], 1, 128), F32),
            pltpu.VMEM((1, 1, 128), F32),
            pltpu.VMEM((sizes[2] * 2, 1, 128), F32),
            dma((MINE,)),
            dma((MINE,)),
            dma((MINE,)),
            dma((3,)),
            dma((3,)),
            dma((3, longest)),
            dma((3, longest)),
            dma((3,)),
            dma((3,)),
            dma(()),
            dma(()),
            dma(()),
            dma(()),
            dma(()),
        ],
        compiler_params=pltpu.CompilerParams(
            collective_id=0, has_side_effects=True, vmem_limit_bytes=60 * 1024 * 1024
        ),
    )(
        ranges,
        strengths,
        live,
        pots,
        counts,
        parents,
        turn_counts,
        reach,
        jnp.asarray(card_rows()),
    )
    return turn_values, total[0, 0]


def solution(mesh):
    sides = {128: (4, 4, 4), 16: (2, 2, 2)}[mesh.devices.size]
    split = Mesh(mesh.devices.reshape(*sides, 2), AXES)
    in_specs = (
        P(NODE, None, "hand"),
        P(NODE, None),
        P(NODE, None),
        P(NODE, None),
        P(NODE),
        P(NODE),
        P(),
        P(None, None, "hand"),
    )
    out_specs = (P(NODE, None, "hand"), P())
    return jax.shard_map(
        functools.partial(local, sides),
        mesh=split,
        in_specs=in_specs,
        out_specs=out_specs,
        check_vma=False,
    )
```

time: 229 us -> 67 us (0.29)
  matrix products: 59.2 us -> 0 us
  Pallas kernels: 0 us -> 53.8 us
  waiting for transfers between devices: 47.1 us -> 0 us
  other arithmetic: 32.8 us -> 0 us
  blocking collectives: 31.7 us -> 0 us
  local copies, waits for them, and re-layouts: 32.7 us -> 10.5 us
  between operations: 14.2 us -> 2.4 us
  starting transfers between devices: 10.2 us -> 0 us
    dot_general x9 -> x0, matrix products: 59.2 us -> none  [the longest x8 58.4 us: showdown_block(): jnp.einsum('nij,nlj->nli', matrix, reach_block, preferred_element_type=jn...]
    pallas_call x0 -> x1, Pallas kernels: none -> 53.8 us  [local(): pl.pallas_call(functools.partial(kernel, sizes), out_shape=(jax.ShapeDtyp...]
    psum x4 -> x0, blocking collectives: 31.7 us -> none  [one_axis_at_a_time(): return functools.reduce(lax.psum, axes, shard)]
    all_gather x1 -> x0, waiting for transfers between devices: 25.3 us -> none  [local(): lax.all_gather(ranges, 'hand', axis=2, tiled=True)]
    all_to_all x1 -> x0, waiting for transfers between devices: 21.1 us -> none  [sent_and_summed(): parts = lax.all_to_all(cut_along(shard, dim, count), axis, 0, 0, tiled=True)]
    reduce_max x2 -> x0, other arithmetic: 16.9 us -> none  [the longest x1 16.8 us: river_from(): jnp.where(usable[:, None, None, :, None], values, -1e+30).max(axis=3)]
    dynamic_slice x13 -> x0, local copies, waits for them, and re-layouts: 16 us -> none  [the longest x8 12.8 us: local(): lax.map(one_block, (grouped(row_strength), grouped(row_live), grouped(str...]
    select_n x8 -> x0, other arithmetic: 12.2 us -> none  [pair_compat(): return jnp.where(shared, 0.0, 1.0).astype(jnp.float32)]
  transfers between devices with their start and end apart: 2 -> 0, of which waited for: 2 -> 0; matrix products, arithmetic and copies ran while one was open for 3% -> 0% of each run, Pallas kernels for 0% -> 0%
where the time goes in v1:
time: 67 us; the launch traced here: 66.6 us
  Pallas kernels  53.8 us (80%)
  local copies, waits for them, and re-layouts  10.5 us (16%)
  between operations  2.4 us (4%)
    pallas_call x1, Pallas kernels, local(): pl.pallas_call(functools.partial(kernel, sizes), out_shape=(jax.ShapeDtyp...  53.8 us
    unnamed x2, local copies, waits for them, and re-layouts  10.5 us

profile of v1, /device:TPU:1, one launch (start us, length us, event | category | flops | bytes accessed | tf_op | source)
XLA Modules:
  0.0 66.6 jit_solution(14992559574230789204)
XLA Ops:
  0.6 9.2 %copy.11.ranges = bf16[32,128,663]{2,1,0:T(8,128)(2,1)} copy(bf16[32,128,663]{1,0,2:T(8,128)(2,1)} %param.9) | data formatting | bytes 10862592 | tf_op args[0]
  9.8 53.8 %shard_map.104 = (f32[1,2,663]{2,1,0:T(2,128)}, f32[1,1]{1,0:T(1,128)}) custom-call(bf16[32,128,663]{2,1,0:T(8,128)(2,1)} %copy.11.ranges, s32[32,1326]{1,0:T(8,128)} %strengths.1, s32[32,1326]{1,0:T(8,128)} %live.1, f32[32,128]{1,0:T(8,128)} %pots.1, s32[32]{0:T(128)} %counts.1, s32[32]{0:T(128)} %parents.1, s32[64]{0:T(128)} %turn_counts.1, ...), custom_call_target="tpu_custom_call" | custom-call | tf_op jit(solution)/shard_map/pallas_call | solution.py:476
  63.6 1.3 %copy.14 = f32[1,2,663]{2,1,0:T(2,128)} copy(f32[1,2,663]{2,1,0:T(2,128)} %get-tuple-element.8) | data formatting | bytes 10608

commit v2 on v1

--- a/solution.py
+++ b/solution.py
@@ -23,18 +23,23 @@
 WIDE = 768
 LOCAL = 32
 MINE = 16
-EARLY = 11
-K_TILES = ((0, 256, 256), (256, 256, 256), (512, 160, 151))
-
-
-def card_rows():
+EARLY = 5
+TALL = 672
+K_TILES = ((0, 256), (256, 256), (512, 160))
+J_BLOCKS = tuple((b * 128, min(128, HALF - b * 128)) for b in range(6))
+
+
+def card_hots():
     first, second = np.triu_indices(52, 1)
-    rows = np.zeros((8, WIDE), np.float32)
+    hots = np.zeros((4, WIDE, 64), np.float32)
     for half in range(2):
-        part = slice(half * HALF, (half + 1) * HALF)
-        rows[half, :HALF] = first[part]
-        rows[2 + half, :HALF] = second[part]
-    return rows
+        for h in range(HALF):
+            cards = [first[half * HALF + h], second[half * HALF + h]]
+            hots[half, h, cards] = 1.0
+            hots[2 + half, h, cards] = -1.0
+            hots[2 + half, h, 52] = 1.0
+        hots[half, :, 52] = 1.0
+    return hots
 
 
 def tall(row, rows):
@@ -45,6 +50,19 @@
 
 def turned(row):
     return jnp.broadcast_to(row, (128, 128)).T
+
+
+def merged(parts, reduce):
+    row = lax.broadcasted_iota(jnp.int32, (8, 128), 0)
+    for bit in (1, 2, 4):
+        low = (row & bit) == 0
+        pairs = []
+        for one, two in zip(parts[::2], parts[1::2]):
+            kept = jnp.where(low, one, two)
+            moved = pltpu.roll(jnp.where(low, two, one), 8 - bit, axis=0)
+            pairs.append(reduce(kept, moved))
+        parts = pairs
+    return parts[0]
 
 
 def kernel(
@@ -57,11 +75,11 @@
     parents,
     turn_counts,
     reach,
-    cards,
+    hots,
     turn_out,
     total_out,
-    own_ranges,
-    other_ranges,
+    raw,
+    by_node,
     masked,
     s_rows,
     live_rows,
@@ -69,7 +87,9 @@
     s_columns,
     allow,
     forbid,
+    pot_columns,
     partial,
+    hot,
     gathered,
     outgoing,
     keys,
@@ -142,12 +162,32 @@
         pl.semaphore_signal(barrier, inc=1, device_id=peer, device_id_type=MESH_ID)
 
     first = core * MINE
-    for n in range(MINE):
-        pltpu.make_async_copy(ranges.at[first + n], own_ranges.at[n], own_sem.at[n]).start()
+    def fetch(block):
+        start, width = J_BLOCKS[block]
+        return pltpu.make_async_copy(
+            ranges.at[pl.ds(start, width), pl.ds(pl.multiple_of(first, MINE), MINE)],
+            raw.at[0, pl.ds(start, width)],
+            own_sem.at[block],
+        )
+
+    def exchange(block):
+        start, width = J_BLOCKS[block]
+        theirs = pl.ds(pl.multiple_of(far * MINE, MINE), MINE)
+        return pltpu.make_async_remote_copy(
+            src_ref=ranges.at[pl.ds(start, width), theirs],
+            dst_ref=raw.at[1, pl.ds(start, width)],
+            send_sem=ranges_send.at[block],
+            recv_sem=other_sem.at[block],
+            device_id=at(place, far),
+            device_id_type=MESH_ID,
+        )
+
+    for block in range(6):
+        fetch(block).start()
     pltpu.make_async_copy(reach.at[turn], my_reach, reach_sem).start()
 
     rows = pl.ds(pl.multiple_of(first, MINE), MINE)
-    s_rows[...] = jnp.zeros_like(s_rows)
+    s_rows[...] = jnp.full_like(s_rows, -1000.0)
     live_rows[...] = jnp.zeros_like(live_rows)
     for source, target, shift in ((strengths, s_rows, 200.0), (live, live_rows, 0.0)):
         low = source[rows, 0:HALF].astype(F32) - shift
@@ -160,83 +200,97 @@
     for n in range(MINE):
         pot_rows[n] = my_pots[n : n + 1]
 
-    def pick(kind, half, lanes):
-        low = cards[pl.ds(2 * kind, 1), lanes]
-        high = cards[pl.ds(2 * kind + 1, 1), lanes]
-        return jnp.where(core == half, low, high)
-
-    lane = lax.broadcasted_iota(jnp.int32, (128, 128), 1)
-    inside = (lane < HALF - 640).astype(F32).astype(BF16)
-
-    def build(block, _):
-        j_lanes = pl.ds(pl.multiple_of(block * 128, 128), 128)
-        for j_half in range(2):
-            a = turned(pick(0, j_half, j_lanes)).astype(BF16)
-            b = turned(pick(1, j_half, j_lanes)).astype(BF16)
-            for i_half in range(2):
-                for i_block in range(6):
-                    lanes = pl.ds(i_block * 128, 128)
-                    c = tall(pick(0, i_half, lanes), 128)
-                    d = tall(pick(1, i_half, lanes), 128)
-                    apart = ((a - c) * (a - d)) * ((b - c) * (b - d))
-                    one = jnp.minimum(jnp.abs(apart), jnp.ones_like(apart))
-                    if i_block == 5:
-                        one = one * inside
-                    where = pl.ds(i_half * WIDE + i_block * 128, 128)
-                    allow[j_half, j_lanes, where] = one
-                    forbid[j_half, j_lanes, where] = -one
+    def build(group, _):
+        lanes = pl.ds(pl.multiple_of(group * 256, 256), 256)
+        for j_half, j_core in enumerate((core, far)):
+            for i_half, i_core in enumerate((core, far)):
+                free = lax.dot_general(
+                    hots[j_core, 0:TALL, :],
+                    hots[2 + i_core, lanes, :],
+                    (((1,), (1,)), ((), ())),
+                    preferred_element_type=F32,
+                ).astype(BF16)
+                for side in range(2):
+                    part = free[:, side * 128 : side * 128 + 128]
+                    zero = jnp.zeros_like(part)
+                    where = i_half * 6 + group * 2 + side
+                    allow[j_half, where] = jnp.maximum(part, zero)
+                    forbid[j_half, where] = jnp.minimum(-part, zero)
         return 0
 
-    lax.fori_loop(0, 6, build, 0)
-
-    def prepare(half, source, n):
+    lax.fori_loop(0, 3, build, 0)
+
+    def swap(half, wait):
+        for block in range(6):
+            wait(block)
+
+        def one(block, _):
+            rows = pl.ds(pl.multiple_of(block * 128, 128), 128)
+            by_node[half, :, rows, :] = jnp.swapaxes(raw[half, rows], 0, 1)
+            return 0
+
+        lax.fori_loop(0, 5, one, 0)
+        by_node[half, :, 640:TALL, :] = jnp.swapaxes(raw[half, 640:TALL], 0, 1)
+
+    lane = lax.broadcasted_iota(jnp.int32, (LINES, 128), 1)
+    action = lax.rem(lax.broadcasted_iota(jnp.int32, (LINES, 128), 0), ACT)
+
+    def prepare(half, n, slot):
         for block in range(6):
             lanes = pl.ds(block * 128, 128)
-            s_columns[lanes, :] = turned(s_rows[half, n, :, lanes]).astype(BF16)
-        for start, _, width in K_TILES:
-            lanes = pl.ds(start, width)
             flags = tall(live_rows[half, n, :, lanes], LINES)
-            masked[:, lanes] = source[n, :, lanes] * flags
-
-    def product(half, n, tile):
-        lanes = pl.ds((tile % 3) * 256, 256)
-        s_lane = s_rows[tile // 3, n, :, lanes]
+            if block < 5:
+                s_columns[slot, lanes, :] = turned(s_rows[half, n, :, lanes].astype(BF16))
+                masked[slot, block] = by_node[half, n, lanes, :].T * flags
+            else:
+                column = turned(s_rows[half, n, :, lanes].astype(BF16))
+                s_columns[slot, 640:TALL, :] = column[: TALL - 640]
+                last = by_node[half, n, 640:TALL, :]
+                last = jnp.concatenate([last, jnp.zeros((96, 128), BF16)], axis=0).T
+                last = (last * flags).astype(F32)
+                bar = jnp.where(action < counts[first + n], 0.0, -1024.0)
+                bar = jnp.where(lane == HALF - 640, bar, 0.0)
+                masked[slot, block] = jnp.where(lane < HALF - 640, last, bar).astype(BF16)
+
+    def product(half, n, slot, tile):
         added = None
-        for start, tall_rows, width in K_TILES:
-            inner = pl.ds(start, tall_rows)
-            column = s_columns[inner, :]
-            gap = tall(s_lane, tall_rows) - jnp.concatenate([column, column], axis=1)
-            where = pl.ds(tile * 256, 256)
-            sign = jnp.minimum(
-                jnp.maximum(gap, forbid[half, inner, where]), allow[half, inner, where]
-            )
+        for step, (start, height) in enumerate(K_TILES):
+            inner = pl.ds(start, height)
+            column = s_columns[slot, inner, :]
+            signs = []
+            for side in range(2):
+                lanes = pl.ds((tile % 3) * 256 + side * 128, 128)
+                gap = tall(s_rows[tile // 3, n, :, lanes], height) - column
+                where = tile * 2 + side
+                signs.append(
+                    jnp.minimum(
+                        jnp.maximum(gap, forbid[half, where, inner, :]),
+                        allow[half, where, inner, :],
+                    )
+                )
+            left = jnp.concatenate([masked[slot, 2 * step], masked[slot, 2 * step + 1]], axis=1)
             term = jnp.dot(
-                masked[:, pl.ds(start, width)], sign[:width], preferred_element_type=F32
+                left[:, :height],
+                jnp.concatenate(signs, axis=1),
+                preferred_element_type=F32,
             )
             added = term if added is None else added + term
         return added
 
-    def own_half(n, _):
-        pltpu.make_async_copy(ranges.at[first + n], own_ranges.at[n], own_sem.at[n]).wait()
-        prepare(0, own_ranges, n)
-        for tile in range(6):
-            partial[n, :, pl.ds(tile * 256, 256)] = product(0, n, tile)
+    def own_half(pair, _):
+        for slot in range(2):
+            prepare(0, 2 * pair + slot, slot)
+        for slot in range(2):
+            n = 2 * pair + slot
+            for tile in range(6):
+                partial[n, :, pl.ds(tile * 256, 256)] = product(0, n, slot, tile)
         return 0
 
-    def exchange(n):
-        return pltpu.make_async_remote_copy(
-            src_ref=ranges.at[far * MINE + n],
-            dst_ref=other_ranges.at[n],
-            send_sem=ranges_send.at[n],
-            recv_sem=other_sem.at[n],
-            device_id=at(place, far),
-            device_id_type=MESH_ID,
-        )
-
+    swap(0, lambda block: fetch(block).wait())
     lax.fori_loop(0, EARLY, own_half, 0)
     pl.semaphore_wait(barrier, len(peers))
-    for n in range(MINE):
-        exchange(n).start()
+    for block in range(6):
+        exchange(block).start()
 
     lane_row = lax.broadcasted_iota(jnp.int32, (1, 128), 1)
     spread = jnp.zeros((1, 128), jnp.int32)
@@ -259,7 +313,8 @@
         for step in range(1, sizes[axis]):
             key_copy(axis, step).start()
 
-    lax.fori_loop(EARLY, MINE, own_half, 0)
+    lax.fori_loop(EARLY, MINE // 2, own_half, 0)
+    swap(1, lambda block: exchange(block).wait_recv())
 
     my_block = core * (MINE * 4)
 
@@ -298,33 +353,27 @@
             )
         return copies
 
-    action = lax.rem(lax.broadcasted_iota(jnp.int32, (LINES, 256), 0), ACT)
-
-    def other_half(n):
-        exchange(n).wait_recv()
-        prepare(1, other_ranges, n)
-        usable = action < counts[first + n]
-        pot = turned(pot_rows[n])
-        pot = jnp.concatenate([pot, pot], axis=1)
-        rivers = []
+    def two_nodes(batch, _):
+        for slot in range(2):
+            n = 2 * batch + slot
+            prepare(1, n, slot)
+            pot_columns[slot] = turned(pot_rows[n])
         for tile in range(6):
-            values = product(1, n, tile) + partial[n, :, pl.ds(tile * 256, 256)]
-            values = jnp.where(usable, values * pot, -1e30)
-            best = values.reshape(2, GROUPS, ACT, 256).max(axis=2).sum(axis=1)
-            best = best * live_rows[tile // 3, n, :, pl.ds((tile % 3) * 256, 256)]
-            rivers.append(best)
-        return rivers
-
-    def two_nodes(batch, _):
-        even, odd = other_half(2 * batch), other_half(2 * batch + 1)
-        for tile in range(6):
-            pieces = []
-            for best in (even[tile], odd[tile]):
+            rows = []
+            for slot in range(2):
+                n = 2 * batch + slot
+                values = product(1, n, slot, tile) + partial[n, :, pl.ds(tile * 256, 256)]
                 for player in range(2):
                     for side in range(2):
-                        lanes = slice(side * 128, side * 128 + 128)
-                        pieces.append(best[player : player + 1, lanes])
-            block = jnp.concatenate(pieces, axis=0)
+                        start = (tile % 3) * 256 + side * 128
+                        parts = []
+                        for g in range(GROUPS):
+                            at_row = (player * GROUPS + g) * ACT
+                            part = values[at_row : at_row + 8, side * 128 : side * 128 + 128]
+                            parts.append(part * pot_columns[slot, at_row : at_row + 8, :])
+                        best = merged(parts, jnp.maximum)
+                        rows.append(best * live_rows[tile // 3, n, :, pl.ds(start, 128)])
+            block = merged(rows, jnp.add)
             if tile < 3:
                 gathered[tile, pl.ds(pl.multiple_of(my_block + batch * 8, 8), 8), :] = block
             else:
@@ -345,22 +394,24 @@
         there = in_plane(axis, q // 16)
         owner = (there[0] * sizes[1] + there[1]) * sizes[2] + there[2]
         wanted = (owner * (TACT * 4) + lax.rem(q, 16)).astype(F32)
+        for e in range(sizes[axis]):
+            hit = jnp.where(wanted == keys[axis, e], 1.0, 0.0).astype(BF16)
+            hot[axis, e, 0 : count * 16, :] = hit
+
+    for axis in range(3):
+        count = plane_size(axis)
         lines = sizes[axis] * 128
-        hot = jnp.concatenate(
-            [
-                jnp.where(wanted == keys[axis, e], 1.0, 0.0).astype(BF16)
-                for e in range(sizes[axis])
-            ],
-            axis=1,
-        )
         blocks = (sizes[axis] - 1) * 128 + 64
         whole = gathered.at[axis, pl.ds(0, blocks)]
         pltpu.make_async_copy(whole, whole, line_recv.at[axis]).wait()
         rows_in = gathered[axis, pl.ds(0, lines), :]
         upper = rows_in.astype(BF16)
         lower = (rows_in - upper.astype(F32)).astype(BF16)
-        both = jnp.dot(hot, upper, preferred_element_type=F32) + jnp.dot(
-            hot, lower, preferred_element_type=F32
+        left = jnp.concatenate(
+            [hot[axis, e, 0 : count * 16, :] for e in range(sizes[axis])], axis=1
+        )
+        both = jnp.dot(left, upper, preferred_element_type=F32) + jnp.dot(
+            left, lower, preferred_element_type=F32
         )
         sums[axis, pl.ds(0, count * 16), :] = both
         mine = plane_mine(axis)
@@ -446,8 +497,8 @@
         second_hop(step, core).start()
         second_hop(step, far).start()
 
-    for n in range(MINE):
-        exchange(n).wait_send()
+    for block in range(6):
+        exchange(block).wait_send()
     for axis in range(3):
         for step in range(1, sizes[axis]):
             key_copy(axis, step).wait_send()
@@ -482,16 +533,18 @@
         in_specs=[hbm, vmem, vmem, vmem, smem, smem, smem, hbm, vmem],
         out_specs=(vmem, smem),
         scratch_shapes=[
-            pltpu.VMEM((MINE, LINES, HALF), BF16),
-            pltpu.VMEM((MINE, LINES, HALF), BF16),
-            pltpu.VMEM((LINES, HALF), BF16),
+            pltpu.VMEM((2, TALL, MINE, LINES), BF16),
+            pltpu.VMEM((2, MINE, TALL, LINES), BF16),
+            pltpu.VMEM((2, 6, LINES, 128), BF16),
             pltpu.VMEM((2, MINE, 1, WIDE), F32),
             pltpu.VMEM((2, MINE, 1, WIDE), F32),
             pltpu.VMEM((MINE, 1, LINES), F32),
-            pltpu.VMEM((WIDE, 128), BF16),
-            pltpu.VMEM((2, WIDE, 2 * WIDE), BF16),
-            pltpu.VMEM((2, WIDE, 2 * WIDE), BF16),
+            pltpu.VMEM((2, TALL, 128), BF16),
+            pltpu.VMEM((2, 12, TALL, 128), BF16),
+            pltpu.VMEM((2, 12, TALL, 128), BF16),
+            pltpu.VMEM((2, LINES, 128), F32),
             pltpu.VMEM((MINE, LINES, 2 * WIDE), F32),
+            pltpu.VMEM((3, longest, widest * 16, 128), BF16),
             pltpu.VMEM((3, longest * 128, 128), F32),
             pltpu.VMEM((3, 64, 128), F32),
             pltpu.VMEM((3, longest, 1, 128), F32),
@@ -502,9 +555,9 @@
             pltpu.VMEM((sizes[0] * sizes[1], 1, 128), F32),
             pltpu.VMEM((1, 1, 128), F32),
             pltpu.VMEM((sizes[2] * 2, 1, 128), F32),
-            dma((MINE,)),
-            dma((MINE,)),
-            dma((MINE,)),
+            dma((6,)),
+            dma((6,)),
+            dma((6,)),
             dma((3,)),
             dma((3,)),
             dma((3, longest)),
@@ -521,7 +574,7 @@
             collective_id=0, has_side_effects=True, vmem_limit_bytes=60 * 1024 * 1024
         ),
     )(
-        ranges,
+        jnp.transpose(ranges, (2, 0, 1)),
         strengths,
         live,
         pots,
@@ -529,7 +582,7 @@
         parents,
         turn_counts,
         reach,
-        jnp.asarray(card_rows()),
+        jnp.asarray(card_hots(), BF16),
     )
     return turn_values, total[0, 0]
 

time: 67 us -> 55.6 us (0.83)
  local copies, waits for them, and re-layouts: 10.5 us -> 1.29 us
  Pallas kernels: 53.8 us -> 51.7 us
    unnamed x2 -> x1, local copies, waits for them, and re-layouts: 10.5 us -> 1.29 us
    pallas_call x1, Pallas kernels: 53.8 us -> 51.7 us  [local(): pl.pallas_call(functools.partial(kernel, sizes), out_shape=(jax.ShapeDtyp...]
where the time goes in v2:
time: 55.6 us; the launch traced here: 55.4 us
  Pallas kernels  51.7 us (93%)
  between operations  2.4 us (4%)
  local copies, waits for them, and re-layouts  1.29 us (2%)
    pallas_call x1, Pallas kernels, local(): pl.pallas_call(functools.partial(kernel, sizes), out_shape=(jax.ShapeDtyp...  51.7 us
    unnamed x1, local copies, waits for them, and re-layouts  1.29 us

profile of v2, /device:TPU:1, one launch (start us, length us, event | category | flops | bytes accessed | tf_op | source)
XLA Modules:
  0.0 55.4 jit_solution(3378225241474278377)
XLA Ops:
  0.6 51.7 %shard_map.104 = (f32[1,2,663]{2,1,0:T(2,128)}, f32[1,1]{1,0:T(1,128)}) custom-call(bf16[663,32,128]{2,1,0:T(8,128)(2,1)} %bitcast.2, s32[32,1326]{1,0:T(8,128)} %strengths.1, s32[32,1326]{1,0:T(8,128)} %live.1, f32[32,128]{1,0:T(8,128)} %pots.1, s32[32]{0:T(128)} %counts.1, s32[32]{0:T(128)} %parents.1, s32[64]{0:T(128)} %turn_counts.1, ...), custom_call_target="tpu_custom_call" | custom-call | tf_op jit(solution)/shard_map/pallas_call | solution.py:527
  52.3 1.3 %copy.13 = f32[1,2,663]{2,1,0:T(2,128)} copy(f32[1,2,663]{2,1,0:T(2,128)} %get-tuple-element.8) | data formatting | bytes 10608
